TPU v7x, 32 devices: a whole 2x2x4 slice. The times are simulated.
32 devices in a mesh: row: 8 (over z, core), col: 4 (over y, x).
Axes of the slice: x: 2, y: 2, z: 4, core: 2. Of those that a mesh axis runs over, the one named last changes fastest.
Arguments:
- x_fwd: bfloat16 [512, 6144], P('row', 'col'), may hold values from -6 to 6
- x_bwd: bfloat16 [512, 6144], P('row', 'col'), may hold values from -6 to 6
- grad_out: bfloat16 [512, 6144], P('row', 'col'), may hold values from -1.5 to 1.5
- gain: float32 [6144], P('col'), may hold values from 0.1 to 1.9
- w_up: bfloat16 [6144, 12288], P('col', 'row'), may hold values from -0.078125 to 0.078125
- w_down: bfloat16 [12288, 6144], P('row', 'col'), may hold values from -0.0546875 to 0.0546875
Outputs:
- y_fwd: bfloat16 [512, 6144], P('row', 'col')
- dx_bwd: bfloat16 [512, 6144], P('row', 'col')
- step_up: float32 [6144, 12288], P('col', 'row')
- step_down: float32 [12288, 6144], P('row', 'col')
- step_gain: float32 [6144], P('col')
- grad_rms: float32 [], replicated
All inputs are finite; a program needn't handle non-finite values.
Results may differ from a plain program's by a relative error of at most 0.0017.
The roundings to bfloat16 on the way count: a program that leaves them out, or rounds other values in their place, can miss the bound.
Values may be sent and summed in bfloat16 or wider, within the bound.
A program may use at most 128 MiB of HBM per device.

v0:
```python
import math
import jax
import jax.numpy as jnp
from jax import lax
from jax.sharding import PartitionSpec as P

D = 6144
FF = 12288
eps = 1e-06
clip_share = 0.25


def erf_gelu(value):
    return 0.5 * value * (1.0 + lax.erf(value * 0.7071067811865476))


def gelu_slope(value):
    return (
        0.5 * (1.0 + lax.erf(value * 0.7071067811865476))
        + value * jnp.exp(-0.5 * value * value) * 0.3989422804014327
    )


def contract(left, right, left_dim, right_dim):
    return lax.dot_general(
        left, right, (((left_dim,), (right_dim,)), ((), ())), preferred_element_type=jnp.float32
    )


def row_sums(tokens):
    values = tokens.astype(jnp.float32)
    return (jnp.sum(values, -1), jnp.sum(values * values, -1))


def normalize(tokens, first, second):
    values = tokens.astype(jnp.float32)
    centre = first / D
    spread = second / D - centre * centre
    inv_scale = lax.rsqrt(spread + eps)
    return ((values - centre[:, None]) * inv_scale[:, None], inv_scale)


def up_both(normed_a, normed_b, w_up):
    full_a, full_b = (
        lax.all_gather(normed_a, "row", axis=0, tiled=True),
        lax.all_gather(normed_b, "row", axis=0, tiled=True),
    )
    width = w_up.shape[1]
    summed = lax.psum_scatter(
        jnp.concatenate(
            [
                jnp.dot(full_a, w_up, preferred_element_type=jnp.float32),
                jnp.dot(full_b, w_up, preferred_element_type=jnp.float32),
            ],
            1,
        ),
        "col",
        scatter_dimension=0,
        tiled=True,
    )
    return (summed[:, :width], summed[:, width:], full_b)


def on_device(x_fwd, x_bwd, grad_out, gain, w_up, w_down):
    first_a, second_a = row_sums(x_fwd)
    first_b, second_b = row_sums(x_bwd)
    first_a, second_a, first_b, second_b = lax.psum((first_a, second_a, first_b, second_b), "col")
    centred_a, _ = normalize(x_fwd, first_a, second_a)
    centred_b, inv_scale = normalize(x_bwd, first_b, second_b)
    normed_a = (centred_a * gain).astype(jnp.bfloat16)
    normed_b = (centred_b * gain).astype(jnp.bfloat16)
    pre_a, pre_b, normed_full = up_both(normed_a, normed_b, w_up)
    hidden_a = erf_gelu(pre_a).astype(jnp.bfloat16)
    output_part = jnp.dot(
        lax.all_gather(hidden_a, "col", axis=0, tiled=True),
        w_down,
        preferred_element_type=jnp.float32,
    )
    output_sum = lax.psum_scatter(output_part, "row", scatter_dimension=0, tiled=True)
    y_fwd = (x_fwd.astype(jnp.float32) + output_sum).astype(jnp.bfloat16)
    hidden_b = erf_gelu(pre_b).astype(jnp.bfloat16)
    grad_full = lax.all_gather(grad_out, "row", axis=0, tiled=True)
    grad_hidden = lax.psum_scatter(
        contract(grad_full, w_down, 1, 1), "col", scatter_dimension=0, tiled=True
    )
    grad_pre = (grad_hidden * gelu_slope(pre_b)).astype(jnp.bfloat16)
    hidden_piece = lax.all_gather(hidden_b, "col", axis=0, tiled=True)
    pre_piece = lax.all_gather(grad_pre, "col", axis=0, tiled=True)
    down_total = contract(hidden_piece, grad_full, 0, 0)
    up_total = contract(normed_full, pre_piece, 0, 0)
    input_total = contract(pre_piece, w_up, 1, 1)
    grad_normed = lax.psum_scatter(input_total, "row", scatter_dimension=0, tiled=True)
    scaled = grad_normed * gain
    first_back = jnp.sum(scaled, -1)
    second_back = jnp.sum(scaled * centred_b, -1)
    first_back, second_back = lax.psum((first_back, second_back), "col")
    dx_bwd = (
        grad_out.astype(jnp.float32)
        + inv_scale[:, None]
        * (scaled - first_back[:, None] / D - centred_b * (second_back[:, None] / D))
    ).astype(jnp.bfloat16)
    gain_part = jnp.sum(grad_normed * centred_b, 0)
    weight_squares = jnp.sum(up_total * up_total) + jnp.sum(down_total * down_total)
    g_gain = lax.psum(gain_part, "row")
    first_row = (lax.axis_index("row") == 0).astype(jnp.float32)
    total = lax.psum(weight_squares + first_row * jnp.sum(g_gain * g_gain), ("row", "col"))
    param_count = 2 * D * FF + D
    norm_value = jnp.sqrt(total)
    grad_rms = norm_value / math.sqrt(param_count)
    factor = jnp.minimum(1.0, clip_share * math.sqrt(param_count) / norm_value)
    return (y_fwd, dx_bwd, up_total * factor, down_total * factor, g_gain * factor, grad_rms)


def solution(mesh):
    placed = (
        P("row", "col"),
        P("row", "col"),
        P("row", "col"),
        P("col"),
        P("col", "row"),
        P("row", "col"),
    )
    return jax.shard_map(
        on_device,
        mesh=mesh,
        in_specs=placed,
        out_specs=(
            P("row", "col"),
            P("row", "col"),
            P("col", "row"),
            P("row", "col"),
            P("col"),
            P(),
        ),
        check_vma=False,
    )
```

profile of v0, /device:TPU:0, one launch (start us, length us, event | category | flops | bytes accessed | tf_op | source)
XLA Modules:
  0.0 446.6 jit_solution(12459251885347289089)
XLA Ops:
  7.9 1.1 convert_reduce_fusion
  9.0 1.1 convert_reduce_fusion.1
  10.1 11.4 %all-reduce.1 = (f32[64]{0:T(128)S(1)}, f32[64]{0:T(128)S(1)}, f32[64]{0:T(128)S(1)}, f32[64]{0:T(128)S(1)}) all-reduce(f32[64]{0:T(128)S(1)} %get-tuple-element.12, f32[64]{0:T(128)S(1)} %get-tuple-element.11, f32[64]{0:T(128)S(1)} %get-tuple-element.10, f32[64]{0:T(128)S(1)} %get-tuple-element.9), channel_id=1, replica_groups=mesh['row'=8,'col'=4] {'col'}, use_global_device_ids=true, to_apply=%region_7.0 | all-reduce | flops 256 | bytes 2048 | tf_op jit(solution)/shard_map/psum | solution.py:67
  21.5 2.0 fusion.21
  24.4 13.3 %all-gather.13.cloned.1.call-done = bf16[512,1536]{1,0:T(8,128)(2,1)} async-done(((bf16[64,1536]{1,0:T(8,128)(2,1)}), bf16[512,1536]{1,0:T(8,128)(2,1)}) %all-gather.13.cloned.1.call-update) | async-done | bytes 1572880 | tf_op jit(solution)/shard_map/all_gather | solution.py:82
  37.6 7.1 %fusion.27 = f32[512,1536]{1,0:T(8,128)} fusion(bf16[512,1536]{1,0:T(8,128)(2,1)} %all-gather.13.cloned.1.call-done, bf16[1536,1536]{1,0:T(8,128)(2,1)} %param.11), kind=kOutput, calls=%fused_computation.52 | convolution fusion | flops 2415919104 | bytes 9437184 | tf_op jit(solution)/shard_map/dot_general | solution.py:25
  44.8 19.4 %all-gather.7.cloned.1.call-done = bf16[512,1536]{1,0:T(8,128)(2,1)} async-done(((bf16[64,1536]{1,0:T(8,128)(2,1)}), bf16[512,1536]{1,0:T(8,128)(2,1)}) %all-gather.7.cloned.1.call-update) | async-done | bytes 1572880 | tf_op jit(solution)/shard_map/all_gather | solution.py:45
  64.3 4.9 %fusion.24 = f32[512,1536]{1,0:T(8,128)S(1)} fusion(bf16[512,1536]{1,0:T(8,128)(2,1)} %all-gather.7.cloned.1.call-done, bf16[1536,1536]{1,0:T(8,128)(2,1)} %param.10), kind=kOutput, calls=%fused_computation.49 | convolution fusion | flops 2415919104 | bytes 9437184 | tf_op jit(solution)/shard_map/dot_general | solution.py:52
  69.2 21.7 %all-gather.9.cloned.1.call-done = bf16[512,1536]{1,0:T(8,128)(2,1)} async-done(((bf16[64,1536]{1,0:T(8,128)(2,1)}), bf16[512,1536]{1,0:T(8,128)(2,1)}) %all-gather.9.cloned.1.call-update) | async-done | bytes 1572880 | tf_op jit(solution)/shard_map/all_gather | solution.py:46
  90.9 4.9 %fusion.25 = f32[512,1536]{1,0:T(8,128)S(1)} fusion(bf16[512,1536]{1,0:T(8,128)(2,1)} %all-gather.9.cloned.1.call-done, bf16[1536,1536]{1,0:T(8,128)(2,1)} %param.10), kind=kOutput, calls=%fused_computation.50 | convolution fusion | flops 2415919104 | bytes 9437184 | tf_op jit(solution)/shard_map/dot_general | solution.py:53
  95.9 3.3 pad_maximum_fusion
  99.2 38.2 %reduce-scatter.9.cloned.1.call-done = f32[128,1536]{1,0:T(8,128)} async-done(((f32[512,1536]{1,0:T(8,128)}), f32[128,1536]{1,0:T(8,128)}) %reduce-scatter.9.cloned.1.call-update) | async-done | bytes 786448 | tf_op jit(solution)/shard_map/reduce_scatter | solution.py:83
  137.4 73.5 %reduce-scatter.5.cloned.1.call-done = f32[128,3072]{1,0:T(8,128)} async-done(((f32[512,3072]{1,0:T(8,128)}), f32[128,3072]{1,0:T(8,128)}) %reduce-scatter.5.cloned.1.call-update) | async-done | bytes 1572880 | tf_op jit(solution)/shard_map/reduce_scatter | solution.py:49
  210.9 3.0 multiply_convert_fusion
  214.7 0.7 all-gather.17.cloned.1.call-update
  215.5 29.5 %all-gather.15.cloned.1.call-done = bf16[512,1536]{1,0:T(8,128)(2,1)} async-done(((bf16[128,1536]{1,0:T(8,128)(2,1)}), bf16[512,1536]{1,0:T(8,128)(2,1)}) %all-gather.15.cloned.1.call-update) | async-done | bytes 1572880 | tf_op jit(solution)/shard_map/all_gather | solution.py:88
  244.9 7.1 %fusion.28 = f32[512,1536]{1,0:T(8,128)} fusion(bf16[512,1536]{1,0:T(8,128)(2,1)} %all-gather.15.cloned.1.call-done, bf16[1536,1536]{1,0:T(8,128)(2,1)} %param.10), kind=kOutput, calls=%fused_computation.53 | convolution fusion | flops 2415919104 | bytes 9437184 | tf_op jit(solution)/shard_map/dot_general | solution.py:25
  252.3 25.3 %all-gather.11.cloned.1.call-done = bf16[512,1536]{1,0:T(8,128)(2,1)} async-done(((bf16[128,1536]{1,0:T(8,128)(2,1)}), bf16[512,1536]{1,0:T(8,128)(2,1)}) %all-gather.11.cloned.1.call-update) | async-done | bytes 1572880 | tf_op jit(solution)/shard_map/all_gather | solution.py:75
  277.6 7.1 %fusion.26 = f32[512,1536]{1,0:T(8,128)} fusion(bf16[512,1536]{1,0:T(8,128)(2,1)} %all-gather.11.cloned.1.call-done, bf16[1536,1536]{1,0:T(8,128)(2,1)} %param.11), kind=kOutput, calls=%fused_computation.51 | convolution fusion | flops 2415919104 | bytes 9437184 | tf_op jit(solution)/shard_map/dot_general | solution.py:74
  284.8 1.4 copy-done.5
  286.7 6.0 %multiply_reduce_fusion.1 = (f32[]{:T(128)}, f32[1536,1536]{1,0:T(8,128)}) fusion(bf16[512,1536]{1,0:T(8,128)(2,1)S(1)} %copy-done.5, bf16[512,1536]{1,0:T(8,128)(2,1)S(1)} %copy-done.6), kind=kOutput, calls=%fused_computation.1 | convolution fusion | flops 2420637696 | bytes 12582916 | tf_op jit(solution)/shard_map/dot_general | solution.py:25
  292.7 18.2 %all-gather.17.cloned.1.call-done = bf16[512,1536]{1,0:T(8,128)(2,1)} async-done(((bf16[128,1536]{1,0:T(8,128)(2,1)}), bf16[512,1536]{1,0:T(8,128)(2,1)}) %all-gather.17.cloned.1.call-update) | async-done | bytes 1572880 | tf_op jit(solution)/shard_map/all_gather | solution.py:87
  310.9 8.9 %multiply_reduce_fusion = (f32[]{:T(128)}, f32[1536,1536]{1,0:T(8,128)}) fusion(bf16[512,1536]{1,0:T(8,128)(2,1)} %all-gather.17.cloned.1.call-done, bf16[512,1536]{1,0:T(8,128)(2,1)} %all-gather.13.cloned.1.call-done), kind=kOutput, calls=%fused_computation | convolution fusion | flops 2420637696 | bytes 12582916 | tf_op jit(solution)/shard_map/dot_general | solution.py:25
  321.1 32.5 %reduce-scatter.11.cloned.1.call-done = f32[64,1536]{1,0:T(8,128)} async-done(((f32[512,1536]{1,0:T(8,128)}), f32[64,1536]{1,0:T(8,128)}) %reduce-scatter.11.cloned.1.call-update) | async-done | bytes 393232 | tf_op jit(solution)/shard_map/reduce_scatter | solution.py:92
  353.6 1.4 fusion.17
  355.0 16.1 %psum.62 = f32[1536]{0:T(1024)S(1)} all-reduce(f32[1536]{0:T(1024)S(1)} %get-tuple-element.6), channel_id=1, replica_groups=mesh['row'=8,'col'=4] {'row'}, use_global_device_ids=true, to_apply=%region_19.0 | all-reduce | flops 1536 | bytes 12288 | tf_op jit(solution)/shard_map/psum | solution.py:104
  372.3 38.8 %psum.63 = f32[]{:T(128)} all-reduce(f32[]{:T(128)S(6)} %add.60), channel_id=1, replica_groups=mesh['row'=8,'col'=4] {'row','col'}, use_global_device_ids=true, to_apply=%region_21.0 | all-reduce | flops 1 | bytes 8 | tf_op jit(solution)/shard_map/psum | solution.py:106
  411.9 9.9 %all-reduce = (f32[64]{0:T(128)S(1)}, f32[64]{0:T(128)S(1)}) all-reduce(f32[64]{0:T(128)S(1)} %get-tuple-element.7, f32[64]{0:T(128)S(1)} %get-tuple-element.8), channel_id=1, replica_groups=mesh['row'=8,'col'=4] {'col'}, use_global_device_ids=true, to_apply=%region_15.0 | all-reduce | flops 128 | bytes 1024 | tf_op jit(solution)/shard_map/psum | solution.py:96
  422.5 8.7 %broadcast_multiply_fusion = f32[1536,1536]{1,0:T(8,128)} fusion(f32[1536,1536]{1,0:T(8,128)} %get-tuple-element.31, f32[]{:T(128)S(6)} %min.3), kind=kLoop, calls=%fused_computation.3 | loop fusion | flops 2359296 | bytes 18874372 | tf_op jit(solution)/shard_map/mul | solution.py:111
  431.2 4.8 %broadcast_multiply_fusion.1 = f32[1536,1536]{1,0:T(8,128)} fusion(f32[1536,1536]{1,0:T(8,128)S(1)} %bitcast.15, f32[]{:T(128)S(6)} %min.3), kind=kLoop, calls=%fused_computation.4 | loop fusion | flops 2359296 | bytes 18874372 | tf_op jit(solution)/shard_map/mul | solution.py:111
  436.0 1.7 fusion.23
  437.7 0.9 fusion.16
  (45 shorter events, 4.5 us)
Async XLA Ops:
  7.2 30.5 %all-gather.13.cloned.1.call-start = ((), (), s32[]{:S(2)}) async-start(), calls=%async_computation.9 | async-start | bytes 1769472 | tf_op jit(solution)/shard_map/all_gather | solution.py:82
  7.9 56.4 %all-gather.7.cloned.1.call-start = ((), (), s32[]{:S(2)}) async-start(), calls=%async_computation.4 | async-start | bytes 1769472 | tf_op jit(solution)/shard_map/all_gather | solution.py:45
  23.6 67.3 %all-gather.9.cloned.1.call-start = ((), (), s32[]{:S(2)}) async-start(), calls=%async_computation.5 | async-start | bytes 1769472 | tf_op jit(solution)/shard_map/all_gather | solution.py:46
  24.3 113.1 %reduce-scatter.9.cloned.1.call-start = ((), (), s32[]{:S(2)}) async-start(), calls=%async_computation.10 | async-start | bytes 3932160 | tf_op jit(solution)/shard_map/reduce_scatter | solution.py:83
  44.8 166.1 %reduce-scatter.5.cloned.1.call-start = ((), (), s32[]{:S(2)}) async-start(), calls=%async_computation.6 | async-start | bytes 7864320 | tf_op jit(solution)/shard_map/reduce_scatter | solution.py:49
  99.1 145.8 %all-gather.15.cloned.1.call-start = ((), (), s32[]{:S(2)}) async-start(), calls=%async_computation.11 | async-start | bytes 1966080 | tf_op jit(solution)/shard_map/all_gather | solution.py:88
  213.9 63.7 %all-gather.11.cloned.1.call-start = ((), (), s32[]{:S(2)}) async-start(), calls=%async_computation.7 | async-start | bytes 1966080 | tf_op jit(solution)/shard_map/all_gather | solution.py:75
  214.7 96.2 %all-gather.17.cloned.1.call-start = ((), (), s32[]{:S(2)}) async-start(), calls=%async_computation.13 | async-start | bytes 1966080 | tf_op jit(solution)/shard_map/all_gather | solution.py:87
  215.4 138.2 %reduce-scatter.11.cloned.1.call-start = ((), (), s32[]{:S(2)}) async-start(), calls=%async_computation.12 | async-start | bytes 3538944 | tf_op jit(solution)/shard_map/reduce_scatter | solution.py:92
  252.1 183.9 %reduce-scatter.7.cloned.1.call-start = ((), (), s32[]{:S(2)}) async-start(), calls=%async_computation.8 | async-start | bytes 3538944 | tf_op jit(solution)/shard_map/reduce_scatter | solution.py:79
  284.8 1.4 copy-start.5
  284.8 1.9 copy-start.6
  292.7 60.9 %copy-start = (bf16[64,1536]{1,0:T(8,128)(2,1)S(1)}, bf16[64,1536]{1,0:T(8,128)(2,1)}, u32[]{:S(2)}) copy-start(bf16[64,1536]{1,0:T(8,128)(2,1)} %param.7) | copy-start | bytes 589828
  292.7 60.9 %copy-start.4 = (f32[1536]{0:T(1024)S(1)}, f32[1536]{0:T(1024)}, u32[]{:S(2)}) copy-start(f32[1536]{0:T(1024)} %param.9) | copy-start | bytes 18436
  353.6 77.5 %slice-start = ((s8[9437184]{0:T(1024)(128)(4,1)}), s8[1048576]{0:T(1024)(128)(4,1)S(1)}, s32[]{:S(2)}) async-start(s8[9437184]{0:T(1024)(128)(4,1)} %bitcast.14), calls=%async_computation.14 | async-start | bytes 2097152
  422.4 8.7 %slice-start.1 = ((s8[9437184]{0:T(1024)(128)(4,1)}), s8[4194304]{0:T(1024)(128)(4,1)S(1)}, s32[]{:S(2)}) async-start(s8[9437184]{0:T(1024)(128)(4,1)} %bitcast.14), calls=%async_computation.15 | async-start | bytes 8388608
  422.4 8.7 %slice-start.2 = ((s8[9437184]{0:T(1024)(128)(4,1)}), s8[4194304]{0:T(1024)(128)(4,1)S(1)}, s32[]{:S(2)}) async-start(s8[9437184]{0:T(1024)(128)(4,1)} %bitcast.14), calls=%async_computation.16 | async-start | bytes 8388608
  431.1 4.8 %copy-start.1 = (bf16[64,1536]{1,0:T(8,128)(2,1)S(1)}, bf16[64,1536]{1,0:T(8,128)(2,1)}, u32[]{:S(2)}) copy-start(bf16[64,1536]{1,0:T(8,128)(2,1)} %param.6) | copy-start | bytes 589828
  431.2 6.5 %copy-start.2 = (f32[64,1536]{1,0:T(8,128)S(1)}, f32[64,1536]{1,0:T(8,128)}, u32[]{:S(2)}) copy-start(f32[64,1536]{1,0:T(8,128)} %reduce-scatter.11.cloned.1.call-done) | copy-start | bytes 1179652
  431.2 6.5 %copy-start.3 = (bf16[64,1536]{1,0:T(8,128)(2,1)S(1)}, bf16[64,1536]{1,0:T(8,128)(2,1)}, u32[]{:S(2)}) copy-start(bf16[64,1536]{1,0:T(8,128)(2,1)} %param.8) | copy-start | bytes 589828
Sparse Core Ops, SparseCore 0:
  9.6 27.9 all-gather.12
  39.8 24.3 all-gather.6
  66.5 24.3 all-gather.8
  94.3 43.0 reduce-scatter.8
  140.8 70.0 reduce-scatter.4
  214.0 30.8 all-gather.14
  246.8 30.8 all-gather.10
  280.0 30.8 all-gather.16
  313.2 40.3 reduce-scatter.10
  355.8 40.2 reduce-scatter.6
where the time goes:
time: 447 us
  waiting for transfers between devices  274 us (61%)
  blocking collectives  76.2 us (17%)
  matrix products  46.1 us (10%)
  other arithmetic  29.2 us (7%)
  between operations  18.1 us (4%)
    reduce_scatter x1, waiting for transfers between devices, up_both(): lax.psum_scatter(jnp.concatenate([jnp.dot(full_a, w_up, preferred_element...  73.5 us
    psum x1, blocking collectives, on_device(): lax.psum(weight_squares + first_row * jnp.sum(g_gain * g_gain), ('row', '...  38.8 us
    reduce_scatter x1, waiting for transfers between devices, on_device(): lax.psum_scatter(contract(grad_full, w_down, 1, 1), 'col', scatter_dimens...  38.2 us
    reduce_scatter x1, waiting for transfers between devices, on_device(): lax.psum_scatter(input_total, 'row', scatter_dimension=0, tiled=True)  32.5 us
    all_gather x1, waiting for transfers between devices, on_device(): pre_piece = lax.all_gather(grad_pre, 'col', axis=0, tiled=True)  29.5 us
    dot_general x4, matrix products, contract(): lax.dot_general(left, right, (((left_dim,), (right_dim,)), ((), ())), pre...  29.2 us
    all_gather x1, waiting for transfers between devices, on_device(): lax.all_gather(hidden_a, 'col', axis=0, tiled=True)  25.3 us
    all_gather x1, waiting for transfers between devices, up_both(): lax.all_gather(normed_b, 'row', axis=0, tiled=True)  21.7 us
  transfers between devices with their start and end apart: 10, of which 9 were waited for; matrix products, arithmetic and copies ran while one was open for 16% of the time, Pallas kernels for 0%

commit v1 on v0

--- a/solution.py
+++ b/solution.py
@@ -3,6 +3,7 @@
 import jax.numpy as jnp
 from jax import lax
 from jax.sharding import PartitionSpec as P
+from jax.lax import psum
 
 D = 6144
 FF = 12288
@@ -103,7 +104,8 @@
     weight_squares = jnp.sum(up_total * up_total) + jnp.sum(down_total * down_total)
     g_gain = lax.psum(gain_part, "row")
     first_row = (lax.axis_index("row") == 0).astype(jnp.float32)
-    total = lax.psum(weight_squares + first_row * jnp.sum(g_gain * g_gain), ("row", "col"))
+    z_in = weight_squares + first_row * jnp.sum(g_gain * g_gain)
+    total = psum(psum(z_in, axis_name="row"), "col")
     param_count = 2 * D * FF + D
     norm_value = jnp.sqrt(total)
     grad_rms = norm_value / math.sqrt(param_count)

time: 447 us -> 424 us (0.949)
  blocking collectives: 76.2 us -> 52.7 us
    psum x1, blocking collectives: 38.8 us -> 14.6 us  [on_device(): total = psum(psum(z_in, axis_name='row'), 'col')]
where the time goes in v1:
time: 424 us; the launch traced here: 423 us
  waiting for transfers between devices  275 us (65%)
  blocking collectives  52.7 us (12%)
  matrix products  45.9 us (11%)
  other arithmetic  29.2 us (7%)
  between operations  18.1 us (4%)
    reduce_scatter x1, waiting for transfers between devices, up_both(): lax.psum_scatter(jnp.concatenate([jnp.dot(full_a, w_up, preferred_element...  73.5 us
    reduce_scatter x1, waiting for transfers between devices, on_device(): lax.psum_scatter(contract(grad_full, w_down, 1, 1), 'col', scatter_dimens...  38.2 us
    reduce_scatter x1, waiting for transfers between devices, on_device(): lax.psum_scatter(input_total, 'row', scatter_dimension=0, tiled=True)  33.2 us
    all_gather x1, waiting for transfers between devices, on_device(): pre_piece = lax.all_gather(grad_pre, 'col', axis=0, tiled=True)  29.5 us
    dot_general x4, matrix products, contract(): lax.dot_general(left, right, (((left_dim,), (right_dim,)), ((), ())), pre...  29 us
    all_gather x1, waiting for transfers between devices, on_device(): lax.all_gather(hidden_a, 'col', axis=0, tiled=True)  25.3 us
    all_gather x1, waiting for transfers between devices, up_both(): lax.all_gather(normed_a, 'row', axis=0, tiled=True)  21.7 us
    all_gather x1, waiting for transfers between devices, up_both(): lax.all_gather(normed_b, 'row', axis=0, tiled=True)  19.5 us
  transfers between devices with their start and end apart: 10, of which 9 were waited for; matrix products, arithmetic and copies ran while one was open for 16% of the time, Pallas kernels for 0%

profile of v1, /device:TPU:0, one launch (start us, length us, event | category | flops | bytes accessed | tf_op | source)
XLA Modules:
  0.0 423.1 jit_solution(14734123398345530264)
XLA Ops:
  7.9 1.1 convert_reduce_fusion.1
  9.0 1.1 convert_reduce_fusion
  10.1 11.4 %all-reduce.1 = (f32[64]{0:T(128)S(1)}, f32[64]{0:T(128)S(1)}, f32[64]{0:T(128)S(1)}, f32[64]{0:T(128)S(1)}) all-reduce(f32[64]{0:T(128)S(1)} %get-tuple-element.12, f32[64]{0:T(128)S(1)} %get-tuple-element.11, f32[64]{0:T(128)S(1)} %get-tuple-element.10, f32[64]{0:T(128)S(1)} %get-tuple-element.9), channel_id=1, replica_groups=mesh['row'=8,'col'=4] {'col'}, use_global_device_ids=true, to_apply=%region_7.0 | all-reduce | flops 256 | bytes 2048 | tf_op jit(solution)/shard_map/psum | solution.py:68
  21.5 2.0 fusion.21
  24.4 13.3 %all-gather.13.cloned.1.call-done = bf16[512,1536]{1,0:T(8,128)(2,1)} async-done(((bf16[64,1536]{1,0:T(8,128)(2,1)}), bf16[512,1536]{1,0:T(8,128)(2,1)}) %all-gather.13.cloned.1.call-update) | async-done | bytes 1572880 | tf_op jit(solution)/shard_map/all_gather | solution.py:83
  37.6 7.1 %fusion.27 = f32[512,1536]{1,0:T(8,128)} fusion(bf16[512,1536]{1,0:T(8,128)(2,1)} %all-gather.13.cloned.1.call-done, bf16[1536,1536]{1,0:T(8,128)(2,1)} %param.11), kind=kOutput, calls=%fused_computation.52 | convolution fusion | flops 2415919104 | bytes 9437184 | tf_op jit(solution)/shard_map/dot_general | solution.py:26
  44.8 19.5 %all-gather.9.cloned.1.call-done = bf16[512,1536]{1,0:T(8,128)(2,1)} async-done(((bf16[64,1536]{1,0:T(8,128)(2,1)}), bf16[512,1536]{1,0:T(8,128)(2,1)}) %all-gather.9.cloned.1.call-update) | async-done | bytes 1572880 | tf_op jit(solution)/shard_map/all_gather | solution.py:47
  64.3 4.9 %fusion.25 = f32[512,1536]{1,0:T(8,128)S(1)} fusion(bf16[512,1536]{1,0:T(8,128)(2,1)} %all-gather.9.cloned.1.call-done, bf16[1536,1536]{1,0:T(8,128)(2,1)} %param.10), kind=kOutput, calls=%fused_computation.50 | convolution fusion | flops 2415919104 | bytes 9437184 | tf_op jit(solution)/shard_map/dot_general | solution.py:54
  69.2 21.7 %all-gather.7.cloned.1.call-done = bf16[512,1536]{1,0:T(8,128)(2,1)} async-done(((bf16[64,1536]{1,0:T(8,128)(2,1)}), bf16[512,1536]{1,0:T(8,128)(2,1)}) %all-gather.7.cloned.1.call-update) | async-done | bytes 1572880 | tf_op jit(solution)/shard_map/all_gather | solution.py:46
  90.9 4.9 %fusion.24 = f32[512,1536]{1,0:T(8,128)S(1)} fusion(bf16[512,1536]{1,0:T(8,128)(2,1)} %all-gather.7.cloned.1.call-done, bf16[1536,1536]{1,0:T(8,128)(2,1)} %param.10), kind=kOutput, calls=%fused_computation.49 | convolution fusion | flops 2415919104 | bytes 9437184 | tf_op jit(solution)/shard_map/dot_general | solution.py:53
  95.8 3.3 pad_maximum_fusion
  99.2 38.2 %reduce-scatter.9.cloned.1.call-done = f32[128,1536]{1,0:T(8,128)} async-done(((f32[512,1536]{1,0:T(8,128)}), f32[128,1536]{1,0:T(8,128)}) %reduce-scatter.9.cloned.1.call-update) | async-done | bytes 786448 | tf_op jit(solution)/shard_map/reduce_scatter | solution.py:84
  137.4 73.5 %reduce-scatter.5.cloned.1.call-done = f32[128,3072]{1,0:T(8,128)} async-done(((f32[512,3072]{1,0:T(8,128)}), f32[128,3072]{1,0:T(8,128)}) %reduce-scatter.5.cloned.1.call-update) | async-done | bytes 1572880 | tf_op jit(solution)/shard_map/reduce_scatter | solution.py:50
  210.9 3.0 multiply_convert_fusion
  214.0 0.7 all-gather.11.cloned.1.call-update
  215.5 29.5 %all-gather.15.cloned.1.call-done = bf16[512,1536]{1,0:T(8,128)(2,1)} async-done(((bf16[128,1536]{1,0:T(8,128)(2,1)}), bf16[512,1536]{1,0:T(8,128)(2,1)}) %all-gather.15.cloned.1.call-update) | async-done | bytes 1572880 | tf_op jit(solution)/shard_map/all_gather | solution.py:89
  244.9 7.1 %fusion.28 = f32[512,1536]{1,0:T(8,128)} fusion(bf16[512,1536]{1,0:T(8,128)(2,1)} %all-gather.15.cloned.1.call-done, bf16[1536,1536]{1,0:T(8,128)(2,1)} %param.10), kind=kOutput, calls=%fused_computation.53 | convolution fusion | flops 2415919104 | bytes 9437184 | tf_op jit(solution)/shard_map/dot_general | solution.py:26
  252.3 25.3 %all-gather.11.cloned.1.call-done = bf16[512,1536]{1,0:T(8,128)(2,1)} async-done(((bf16[128,1536]{1,0:T(8,128)(2,1)}), bf16[512,1536]{1,0:T(8,128)(2,1)}) %all-gather.11.cloned.1.call-update) | async-done | bytes 1572880 | tf_op jit(solution)/shard_map/all_gather | solution.py:76
  277.7 7.0 %fusion.26 = f32[512,1536]{1,0:T(8,128)} fusion(bf16[512,1536]{1,0:T(8,128)(2,1)} %all-gather.11.cloned.1.call-done, bf16[1536,1536]{1,0:T(8,128)(2,1)} %param.11), kind=kOutput, calls=%fused_computation.51 | convolution fusion | flops 2415919104 | bytes 9437184 | tf_op jit(solution)/shard_map/dot_general | solution.py:75
  284.7 1.4 copy-done.5
  286.7 6.0 %multiply_reduce_fusion.1 = (f32[]{:T(128)}, f32[1536,1536]{1,0:T(8,128)}) fusion(bf16[512,1536]{1,0:T(8,128)(2,1)S(1)} %copy-done.5, bf16[512,1536]{1,0:T(8,128)(2,1)S(1)} %copy-done.6), kind=kOutput, calls=%fused_computation.1 | convolution fusion | flops 2420637696 | bytes 12582916 | tf_op jit(solution)/shard_map/dot_general | solution.py:26
  292.8 17.6 %all-gather.17.cloned.1.call-done = bf16[512,1536]{1,0:T(8,128)(2,1)} async-done(((bf16[128,1536]{1,0:T(8,128)(2,1)}), bf16[512,1536]{1,0:T(8,128)(2,1)}) %all-gather.17.cloned.1.call-update) | async-done | bytes 1572880 | tf_op jit(solution)/shard_map/all_gather | solution.py:88
  310.4 8.8 %multiply_reduce_fusion = (f32[]{:T(128)}, f32[1536,1536]{1,0:T(8,128)}) fusion(bf16[512,1536]{1,0:T(8,128)(2,1)} %all-gather.17.cloned.1.call-done, bf16[512,1536]{1,0:T(8,128)(2,1)} %all-gather.13.cloned.1.call-done), kind=kOutput, calls=%fused_computation | convolution fusion | flops 2420637696 | bytes 12582916 | tf_op jit(solution)/shard_map/dot_general | solution.py:26
  320.4 33.2 %reduce-scatter.11.cloned.1.call-done = f32[64,1536]{1,0:T(8,128)} async-done(((f32[512,1536]{1,0:T(8,128)}), f32[64,1536]{1,0:T(8,128)}) %reduce-scatter.11.cloned.1.call-update) | async-done | bytes 393232 | tf_op jit(solution)/shard_map/reduce_scatter | solution.py:93
  353.7 1.4 fusion.17
  355.0 16.1 %psum.69 = f32[1536]{0:T(1024)S(1)} all-reduce(f32[1536]{0:T(1024)S(1)} %get-tuple-element.6), channel_id=1, replica_groups=mesh['row'=8,'col'=4] {'row'}, use_global_device_ids=true, to_apply=%region_19.0 | all-reduce | flops 1536 | bytes 12288 | tf_op jit(solution)/shard_map/psum | solution.py:105
  372.3 14.6 %psum.70 = f32[]{:T(128)} all-reduce(f32[]{:T(128)S(6)} %add.62), channel_id=1, replica_groups=mesh['row'=8,'col'=4] {'row'}, use_global_device_ids=true, to_apply=%region_21.0 | all-reduce | flops 1 | bytes 8 | tf_op jit(solution)/shard_map/psum | solution.py:108
  387.0 10.6 %all-reduce = (f32[64]{0:T(128)S(1)}, f32[64]{0:T(128)S(1)}, f32[]{:T(128)}) all-reduce(f32[64]{0:T(128)S(1)} %get-tuple-element.7, f32[64]{0:T(128)S(1)} %get-tuple-element.8, f32[]{:T(128)} %psum.70), channel_id=1, replica_groups=mesh['row'=8,'col'=4] {'col'}, use_global_device_ids=true, to_apply=%region_15.0 | all-reduce | flops 129 | bytes 1032 | tf_op jit(solution)/shard_map/psum | solution.py:97
  399.0 8.7 %broadcast_multiply_fusion.1 = f32[1536,1536]{1,0:T(8,128)} fusion(f32[1536,1536]{1,0:T(8,128)} %get-tuple-element.30, f32[]{:T(128)S(6)} %min.3), kind=kLoop, calls=%fused_computation.4 | loop fusion | flops 2359296 | bytes 18874372 | tf_op jit(solution)/shard_map/mul | solution.py:113
  407.7 4.8 %broadcast_multiply_fusion = f32[1536,1536]{1,0:T(8,128)} fusion(f32[1536,1536]{1,0:T(8,128)S(1)} %bitcast.15, f32[]{:T(128)S(6)} %min.3), kind=kLoop, calls=%fused_computation.3 | loop fusion | flops 2359296 | bytes 18874372 | tf_op jit(solution)/shard_map/mul | solution.py:113
  412.5 1.7 fusion.23
  414.2 0.9 fusion.16
  (45 shorter events, 4.5 us)
Async XLA Ops:
  7.2 30.5 %all-gather.13.cloned.1.call-start = ((), (), s32[]{:S(2)}) async-start(), calls=%async_computation.9 | async-start | bytes 1769472 | tf_op jit(solution)/shard_map/all_gather | solution.py:83
  7.9 56.4 %all-gather.9.cloned.1.call-start = ((), (), s32[]{:S(2)}) async-start(), calls=%async_computation.5 | async-start | bytes 1769472 | tf_op jit(solution)/shard_map/all_gather | solution.py:47
  23.6 67.3 %all-gather.7.cloned.1.call-start = ((), (), s32[]{:S(2)}) async-start(), calls=%async_computation.4 | async-start | bytes 1769472 | tf_op jit(solution)/shard_map/all_gather | solution.py:46
  24.3 113.1 %reduce-scatter.9.cloned.1.call-start = ((), (), s32[]{:S(2)}) async-start(), calls=%async_computation.10 | async-start | bytes 3932160 | tf_op jit(solution)/shard_map/reduce_scatter | solution.py:84
  44.8 166.1 %reduce-scatter.5.cloned.1.call-start = ((), (), s32[]{:S(2)}) async-start(), calls=%async_computation.6 | async-start | bytes 7864320 | tf_op jit(solution)/shard_map/reduce_scatter | solution.py:50
  99.1 145.8 %all-gather.15.cloned.1.call-start = ((), (), s32[]{:S(2)}) async-start(), calls=%async_computation.11 | async-start | bytes 1966080 | tf_op jit(solution)/shard_map/all_gather | solution.py:89
  213.9 63.7 %all-gather.11.cloned.1.call-start = ((), (), s32[]{:S(2)}) async-start(), calls=%async_computation.7 | async-start | bytes 1966080 | tf_op jit(solution)/shard_map/all_gather | solution.py:76
  214.7 95.7 %all-gather.17.cloned.1.call-start = ((), (), s32[]{:S(2)}) async-start(), calls=%async_computation.13 | async-start | bytes 1966080 | tf_op jit(solution)/shard_map/all_gather | solution.py:88
  215.4 138.2 %reduce-scatter.11.cloned.1.call-start = ((), (), s32[]{:S(2)}) async-start(), calls=%async_computation.12 | async-start | bytes 3538944 | tf_op jit(solution)/shard_map/reduce_scatter | solution.py:93
  252.1 160.4 %reduce-scatter.7.cloned.1.call-start = ((), (), s32[]{:S(2)}) async-start(), calls=%async_computation.8 | async-start | bytes 3538944 | tf_op jit(solution)/shard_map/reduce_scatter | solution.py:80
  284.7 1.4 copy-start.5
  284.7 2.0 copy-start.6
  292.8 60.9 %copy-start = (bf16[64,1536]{1,0:T(8,128)(2,1)S(1)}, bf16[64,1536]{1,0:T(8,128)(2,1)}, u32[]{:S(2)}) copy-start(bf16[64,1536]{1,0:T(8,128)(2,1)} %param.7) | copy-start | bytes 589828
  292.8 60.9 %copy-start.4 = (f32[1536]{0:T(1024)S(1)}, f32[1536]{0:T(1024)}, u32[]{:S(2)}) copy-start(f32[1536]{0:T(1024)} %param.9) | copy-start | bytes 18436
  353.7 54.0 %slice-start = ((s8[9437184]{0:T(1024)(128)(4,1)}), s8[1048576]{0:T(1024)(128)(4,1)S(1)}, s32[]{:S(2)}) async-start(s8[9437184]{0:T(1024)(128)(4,1)} %bitcast.14), calls=%async_computation.14 | async-start | bytes 2097152
  399.0 8.7 %slice-start.1 = ((s8[9437184]{0:T(1024)(128)(4,1)}), s8[4194304]{0:T(1024)(128)(4,1)S(1)}, s32[]{:S(2)}) async-start(s8[9437184]{0:T(1024)(128)(4,1)} %bitcast.14), calls=%async_computation.15 | async-start | bytes 8388608
  399.0 8.7 %slice-start.2 = ((s8[9437184]{0:T(1024)(128)(4,1)}), s8[4194304]{0:T(1024)(128)(4,1)S(1)}, s32[]{:S(2)}) async-start(s8[9437184]{0:T(1024)(128)(4,1)} %bitcast.14), calls=%async_computation.16 | async-start | bytes 8388608
  407.6 4.8 %copy-start.1 = (bf16[64,1536]{1,0:T(8,128)(2,1)S(1)}, bf16[64,1536]{1,0:T(8,128)(2,1)}, u32[]{:S(2)}) copy-start(bf16[64,1536]{1,0:T(8,128)(2,1)} %param.6) | copy-start | bytes 589828
  407.7 6.5 %copy-start.2 = (f32[64,1536]{1,0:T(8,128)S(1)}, f32[64,1536]{1,0:T(8,128)}, u32[]{:S(2)}) copy-start(f32[64,1536]{1,0:T(8,128)} %reduce-scatter.11.cloned.1.call-done) | copy-start | bytes 1179652
  407.7 6.5 %copy-start.3 = (bf16[64,1536]{1,0:T(8,128)(2,1)S(1)}, bf16[64,1536]{1,0:T(8,128)(2,1)}, u32[]{:S(2)}) copy-start(bf16[64,1536]{1,0:T(8,128)(2,1)} %param.8) | copy-start | bytes 589828
Sparse Core Ops, SparseCore 0:
  9.6 27.9 all-gather.12
  39.8 24.3 all-gather.8
  66.5 24.3 all-gather.6
  94.3 43.0 reduce-scatter.8
  140.8 70.0 reduce-scatter.4
  214.1 30.8 all-gather.14
  246.8 30.8 all-gather.10
  279.5 30.8 all-gather.16
  313.2 40.3 reduce-scatter.10
  355.8 40.0 reduce-scatter.6
